TPU v7x, 32 devices: a whole 2x2x4 slice. The times are simulated.
32 devices in a mesh: gx: 4 (over z), gy: 4 (over x, core), gz: 2 (over y).
Axes of the slice: x: 2, y: 2, z: 4, core: 2. Of those that a mesh axis runs over, the one named last changes fastest.
Arguments:
- volume: int32 [32, 64, 256], P('gx', 'gy', 'gz'), may hold values from 0 to 255
- transfer_table: float32 [4, 256], replicated, may hold values from 0 to 1
- depth_rank: int32 [4], replicated, may hold values from 0 to 3, each once
- footprint: int32 [4, 4, 2, 4], P('gx', 'gy', 'gz'), may hold values from 0 to 128, as said below
Outputs:
- rendered: float32 [4, 64, 256], P(None, 'gy', 'gz')
Inputs may be any that keep to these rules, and one draw needn't show every extreme that they name: depth_rank holds each of 0 to 4 - 1 once. `footprint`: for every brick, entry 0 is below 8 and entry 1 above it, up to 16; entry 2 is below 64 and entry 3 above it, up to 128.
All inputs are finite; a program needn't handle non-finite values.
Results may differ from a plain program's by a relative error of at most 0.0003.
Values sent between devices are 32-bit elements; how exact they have to be, the bound alone decides.
No kernel may reach another device: no remote copies, remote signals or barrier semaphores. Data moves between devices by JAX's collectives and lax.ppermute only.
A program may use at most 64 MiB of HBM per device.

v0:
```python
import jax
import jax.numpy as jnp
from jax import lax
from jax.sharding import PartitionSpec as P

light_x = 1.0 / 3.0
light_y = 2.0 / 3.0
light_z = 2.0 / 3.0


def with_halo(cells, sides, width):
    for axis, dim in sides:
        count = lax.axis_size(axis)
        ends = count - 1
        head = lax.slice_in_dim(cells, 0, width, axis=dim)
        tail = lax.slice_in_dim(cells, cells.shape[dim] - width, cells.shape[dim], axis=dim)
        cells = jnp.concatenate(
            [
                lax.ppermute(tail, axis, [(i, (i + 1) % count) for i in range(ends)]),
                cells,
                lax.ppermute(head, axis, [((i + 1) % count, i) for i in range(ends)]),
            ],
            axis=dim,
        )
    return cells


def shading(lower_plane, upper_plane, padded):
    grad_x = 0.5 * (upper_plane - lower_plane)
    grad_y = 0.5 * (padded[2:, 1:-1] - padded[:-2, 1:-1])
    grad_z = 0.5 * (padded[1:-1, 2:] - padded[1:-1, :-2])
    facing = jnp.abs(grad_x * light_x + grad_y * light_y + grad_z * light_z) / jnp.sqrt(
        1.0 + (grad_x * grad_x + grad_y * grad_y + grad_z * grad_z)
    )
    return 0.35 + 0.65 * facing


def composite(layers, depth_rank):
    order = jnp.argsort(depth_rank)
    ordered = jnp.take(layers, order, axis=0)

    def blend(state_pair, front_layer):
        colour, alpha = state_pair
        cover = 1.0 - alpha
        return ((colour + cover * front_layer[:3], alpha + cover * front_layer[3]), None)

    start_pair = (
        jnp.zeros((3,) + layers.shape[2:], jnp.float32),
        jnp.zeros(layers.shape[2:], jnp.float32),
    )
    (colour, alpha), unused = lax.scan(blend, start_pair, ordered)
    return jnp.concatenate([colour, alpha[None]], axis=0)


def on_device(volume, transfer_table, depth_rank, footprint):
    slab_depth, rows_here, cols_here = volume.shape
    columns = lax.axis_size("gx")
    extent = 4.0 / (slab_depth * columns)
    looked = jnp.take(transfer_table, volume, axis=1)
    density = looked[3]
    emission = looked[:3]
    padded = with_halo(density, (("gx", 0), ("gy", 1), ("gz", 2)), 1)

    def advance(state_pair, offset):
        colour, transmit = state_pair
        window = lax.dynamic_slice_in_dim(padded, offset, 3, 0)
        centre = window[1, 1:-1, 1:-1]
        shading_term = shading(window[0, 1:-1, 1:-1], window[2, 1:-1, 1:-1], window[1])
        emitted = lax.dynamic_index_in_dim(emission, offset, 1, keepdims=False) * shading_term
        sample_alpha = 1.0 - jnp.exp(-extent * centre)
        colour = colour + transmit * sample_alpha * emitted
        transmit = transmit * (1.0 - sample_alpha)
        return ((colour, transmit), None)

    start_pair = (
        jnp.zeros((3, rows_here, cols_here), jnp.float32),
        jnp.ones((rows_here, cols_here), jnp.float32),
    )
    (colour, transmit), unused = lax.scan(
        advance, start_pair, jnp.arange(slab_depth, dtype=jnp.int32)
    )
    rect = footprint[0, 0, 0]
    rows_local = jnp.arange(rows_here, dtype=jnp.int32)[:, None]
    cols_local = jnp.arange(cols_here, dtype=jnp.int32)[None, :]
    inside = (
        (rows_local >= rect[0])
        & (rows_local < rect[1])
        & (cols_local >= rect[2])
        & (cols_local < rect[3])
    )
    layer = jnp.concatenate([colour, (1.0 - transmit)[None]], axis=0)
    partial_value = jnp.where(inside[None], layer, 0.0)[None]
    layers = lax.all_gather(partial_value, "gx", axis=0, tiled=True)
    rendered = composite(layers, depth_rank)
    return rendered


def solution(mesh):
    placed = (P("gx", "gy", "gz"), P(), P(), P("gx", "gy", "gz", None))
    return jax.shard_map(
        on_device, mesh=mesh, in_specs=placed, out_specs=P(None, "gy", "gz"), check_vma=False
    )
```

profile of v0, /device:TPU:0, one launch (start us, length us, event | category | flops | bytes accessed | tf_op | source)
XLA Modules:
  0.0 137.6 jit_solution(11093514029266378517)
XLA Ops:
  0.0 0.9 compare_select_fusion
  0.9 0.9 compare_and_fusion
  1.8 0.8 copy.8
  2.6 54.5 %gather_fusion = f32[16384,4]{1,0:T(8,128)} fusion(f32[4,256]{0,1:T(8,128)S(1)} %copy.8, s32[16384]{0:T(1024)S(1)} %broadcast_clamp_fusion), kind=kCustom, calls=%fused_computation | custom fusion | bytes 589824 | tf_op jit(solution)/shard_map/jit(_take)/gather | solution.py:59
  57.1 5.2 %copy.9 = f32[8,16,128,4]{2,1,3,0:T(8,128)S(1)} copy(f32[8,16,128,4]{3,2,1,0:T(8,128)} %bitcast.81) | data formatting | bytes 524288 | tf_op jit(solution)/shard_map/jit(_take)/gather | solution.py:59
  62.4 5.0 %collective-permute-start = (f32[1,16,128]{2,1,0:T(8,128)S(1)}, f32[1,16,128]{2,1,0:T(8,128)S(1)}, u32[]{:S(2)}, u32[]{:S(2)}) collective-permute-start(f32[1,16,128]{2,1,0:T(8,128)S(1)} %get-tuple-element.194), channel_id=1, source_target_pairs={{0,8},{8,16},{16,24},{1,9},{9,17},{17,25},{2,10},{10,18},{18,26},{... | collective-permute-start | bytes 24584 | tf_op jit(solution)/shard_map/ppermute | solution.py:19
  67.3 1.3 collective-permute-start.1
  68.6 0.0 copy-done
  68.6 0.7 fusion.18
  69.3 1.3 iota_compare_fusion
  70.6 1.3 compare_and_fusion.1
  71.8 0.0 copy-done.1
  71.9 0.7 sort.17
  72.6 0.1 and_and_fusion
  72.7 0.0 collective-permute-done
  72.7 0.2 collective-permute-done.1
  72.9 1.3 collective-permute-start.2
  74.2 1.3 collective-permute-start.3
  75.5 0.0 collective-permute-done.2
  75.5 3.4 %collective-permute-done.3 = f32[10,1,128]{2,1,0:T(1,128)S(1)} collective-permute-done((f32[10,1,128]{2,1,0:T(1,128)S(1)}, f32[10,1,128]{2,1,0:T(1,128)S(1)}, u32[]{:S(2)}, u32[]{:S(2)}) %collective-permute-start.3) | collective-permute-done | bytes 5152 | tf_op jit(solution)/shard_map/ppermute | solution.py:21
  79.0 0.1 fusion.17
  79.1 3.4 %collective-permute-start.4 = (f32[10,18,1]{2,1,0:T(8,128)S(1)}, f32[10,18,1]{2,1,0:T(8,128)S(1)}, u32[]{:S(2)}, u32[]{:S(2)}) collective-permute-start(f32[10,18,1]{2,1,0:T(8,128)S(1)} %get-tuple-element.196), channel_id=1, source_target_pairs={{0,1},{2,3},{4,5},{6,7},{8,9},{10,11},{12,13},{14,15},{16,17},{18,... | collective-permute-start | bytes 2168 | tf_op jit(solution)/shard_map/ppermute | solution.py:19
  82.5 1.3 collective-permute-start.5
  83.9 1.0 collective-permute-done.4
  84.9 4.5 %collective-permute-done.5 = f32[10,18,1]{2,1,0:T(8,128)S(1)} collective-permute-done((f32[10,18,1]{2,1,0:T(8,128)S(1)}, f32[10,18,1]{2,1,0:T(8,128)S(1)}, u32[]{:S(2)}, u32[]{:S(2)}) %collective-permute-start.5) | collective-permute-done | bytes 752 | tf_op jit(solution)/shard_map/ppermute | solution.py:21
  89.5 0.2 pad_maximum_fusion
  89.7 31.6 %while.29 = (s32[]{:T(128)}, f32[3,16,128]{2,1,0:T(8,128)S(1)}, f32[16,128]{1,0:T(8,128)S(1)}, s32[8]{0:T(128)S(1)}, f32[10,18,130]{2,1,0:T(8,128)S(1)}, /*index...) while((s32[]{:T(128)}, f32[3,16,128]{2,1,0:T(8,128)S(1)}, ...), condition=%wide.region_2.3_spmd.clone, body=%wide.region_1.2_spmd.clone.sunk | while | flops 79883 | bytes 199203 | solution.py:79
  89.7 0.6 dynamic_slice.35
  92.3 0.1 subtract_multiply_fusion.2
  93.7 0.6 dynamic_slice.35
  96.2 0.1 subtract_multiply_fusion.2
  97.6 0.6 dynamic_slice.35
  100.2 0.1 subtract_multiply_fusion.2
  101.6 0.6 dynamic_slice.35
  104.1 0.1 subtract_multiply_fusion.2
  105.5 0.6 dynamic_slice.35
  108.1 0.1 subtract_multiply_fusion.2
  109.5 0.6 dynamic_slice.35
  112.0 0.1 subtract_multiply_fusion.2
  113.4 0.6 dynamic_slice.35
  116.0 0.1 subtract_multiply_fusion.2
  117.4 0.6 dynamic_slice.35
  119.9 0.1 subtract_multiply_fusion.2
  121.3 14.8 %all_gather.3 = f32[4,4,16,128]{3,2,1,0:T(8,128)S(1)} all-gather(f32[1,4,16,128]{3,2,1,0:T(8,128)S(1)} %maximum_select_fusion), channel_id=1, replica_groups=mesh['gx'=4,'gy'=4,'gz'=2] {'gx'}, dimensions={0}, use_global_device_ids=true | all-gather | bytes 163840 | tf_op jit(solution)/shard_map/all_gather | solution.py:93
  136.1 0.6 gather_fusion.1
  136.7 0.1 broadcast_select_fusion
  136.8 0.2 while.30
  137.0 0.6 pad_maximum_fusion.2
  (44 shorter events, 0.4 us)
Async XLA Ops:
  0.0 68.6 %copy-start = (s32[1,1,1,4]{3,2,1,0:T(1,128)S(1)}, s32[1,1,1,4]{3,2,1,0:T(1,128)}, u32[]{:S(2)}) copy-start(s32[1,1,1,4]{3,2,1,0:T(1,128)} %param.11) | copy-start | bytes 52
  0.0 71.8 %copy-start.1 = (s32[4]{0:T(128)S(1)}, s32[4]{0:T(128)}, u32[]{:S(2)}) copy-start(s32[4]{0:T(128)} %param.10) | copy-start | bytes 52
  62.4 10.3 %collective-permute-start = (f32[1,16,128]{2,1,0:T(8,128)S(1)}, f32[1,16,128]{2,1,0:T(8,128)S(1)}, u32[]{:S(2)}, u32[]{:S(2)}) collective-permute-start(f32[1,16,128]{2,1,0:T(8,128)S(1)} %get-tuple-element.194), channel_id=1, source_target_pairs={{0,8},{8,16},{16,24},{1,9},{9,17},{17,25},{2,10},{10,18},{18,26},{... | collective-permute-start | bytes 24584 | tf_op jit(solution)/shard_map/ppermute | solution.py:19
  67.3 5.5 %collective-permute-start.1 = (f32[1,16,128]{2,1,0:T(8,128)S(1)}, f32[1,16,128]{2,1,0:T(8,128)S(1)}, u32[]{:S(2)}, u32[]{:S(2)}) collective-permute-start(f32[1,16,128]{2,1,0:T(8,128)S(1)} %get-tuple-element.195), channel_id=1, source_target_pairs={{8,0},{16,8},{24,16},{9,1},{17,9},{25,17},{10,2},{18,10},{26,18},{... | collective-permute-start | bytes 24584 | tf_op jit(solution)/shard_map/ppermute | solution.py:21
  72.9 2.6 %collective-permute-start.2 = (f32[10,1,128]{2,1,0:T(1,128)S(1)}, f32[10,1,128]{2,1,0:T(1,128)S(1)}, u32[]{:S(2)}, u32[]{:S(2)}) collective-permute-start(f32[10,1,128]{2,1,0:T(1,128)S(1)} %get-tuple-element.198), channel_id=1, source_target_pairs={{0,2},{2,4},{4,6},{1,3},{3,5},{5,7},{8,10},{10,12},{12,14},{9,11},... | collective-permute-start | bytes 15368 | tf_op jit(solution)/shard_map/ppermute | solution.py:19
  74.2 4.8 %collective-permute-start.3 = (f32[10,1,128]{2,1,0:T(1,128)S(1)}, f32[10,1,128]{2,1,0:T(1,128)S(1)}, u32[]{:S(2)}, u32[]{:S(2)}) collective-permute-start(f32[10,1,128]{2,1,0:T(1,128)S(1)} %get-tuple-element.199), channel_id=1, source_target_pairs={{2,0},{4,2},{6,4},{3,1},{5,3},{7,5},{10,8},{12,10},{14,12},{11,9},... | collective-permute-start | bytes 15368 | tf_op jit(solution)/shard_map/ppermute | solution.py:21
  79.1 5.9 %collective-permute-start.4 = (f32[10,18,1]{2,1,0:T(8,128)S(1)}, f32[10,18,1]{2,1,0:T(8,128)S(1)}, u32[]{:S(2)}, u32[]{:S(2)}) collective-permute-start(f32[10,18,1]{2,1,0:T(8,128)S(1)} %get-tuple-element.196), channel_id=1, source_target_pairs={{0,1},{2,3},{4,5},{6,7},{8,9},{10,11},{12,13},{14,15},{16,17},{18,... | collective-permute-start | bytes 2168 | tf_op jit(solution)/shard_map/ppermute | solution.py:19
  82.5 7.0 %collective-permute-start.5 = (f32[10,18,1]{2,1,0:T(8,128)S(1)}, f32[10,18,1]{2,1,0:T(8,128)S(1)}, u32[]{:S(2)}, u32[]{:S(2)}) collective-permute-start(f32[10,18,1]{2,1,0:T(8,128)S(1)} %get-tuple-element.197), channel_id=1, source_target_pairs={{1,0},{3,2},{5,4},{7,6},{9,8},{11,10},{13,12},{15,14},{17,16},{19,... | collective-permute-start | bytes 2168 | tf_op jit(solution)/shard_map/ppermute | solution.py:21
where the time goes:
time: 138 us
  local copies, waits for them, and re-layouts  67 us (49%)
  loops' own time  25.6 us (19%)
  blocking collectives  14.8 us (11%)
  starting transfers between devices  13.6 us (10%)
  waiting for transfers between devices  9.22 us (7%)
  other arithmetic  7.12 us (5%)
    gather x2, local copies, waits for them, and re-layouts, on_device(): looked = jnp.take(transfer_table, volume, axis=1)  59.7 us
    another operation x1, loops' own time, on_device(): lax.scan(advance, start_pair, jnp.arange(slab_depth, dtype=jnp.int32))  25.5 us
    all_gather x1, blocking collectives, on_device(): layers = lax.all_gather(partial_value, 'gx', axis=0, tiled=True)  14.8 us
    ppermute x3, starting transfers between devices, with_halo(): lax.ppermute(tail, axis, [(i, (i + 1) % count) for i in range(ends)])  9.69 us
    ppermute x3, waiting for transfers between devices, with_halo(): lax.ppermute(head, axis, [((i + 1) % count, i) for i in range(ends)])  8.17 us
    dynamic_slice x8, local copies, waits for them, and re-layouts, on_device(): lax.scan(advance, start_pair, jnp.arange(slab_depth, dtype=jnp.int32))  5.09 us
    ppermute x3, starting transfers between devices, with_halo(): lax.ppermute(head, axis, [((i + 1) % count, i) for i in range(ends)])  3.88 us
  transfers between devices with their start and end apart: 6, of which 4 were waited for; matrix products, arithmetic and copies ran while one was open for 3% of the time, Pallas kernels for 0%

commit v1 on v0

v1 whole, which is shorter than its diff:
```python
import functools

import jax
import jax.numpy as jnp
from jax import lax
from jax.experimental import pallas as pl
from jax.experimental.pallas import tpu as pltpu
from jax.sharding import PartitionSpec as P

AXES = ("gx", "gy", "gz")
LANES = 128
LIGHT = (1.0 / 3.0, 2.0 / 3.0, 2.0 / 3.0)
SMALL_VMEM = 4 * 1024 * 1024


def partner(index, count, step):
    other = index + 1 if index % 2 == step else index - 1
    return other if 0 <= other < count else None


def swap_pairs(sizes, axis, step):
    pairs = []
    for x in range(sizes[0]):
        for y in range(sizes[1]):
            for z in range(sizes[2]):
                here = [x, y, z]
                there = list(here)
                other = partner(here[axis], sizes[axis], step)
                if other is not None:
                    there[axis] = other
                elif axis == 1 and sizes[1] % 2 == 0:
                    there[1] = sizes[1] - 1 - y
                elif axis != 1 and sizes[1] % 2 == 0:
                    there[1] = y ^ 1
                flat = [(a * sizes[1] + b) * sizes[2] + c for a, b, c in (here, there)]
                pairs.append(tuple(flat))
    return pairs


def swaps_of(sizes):
    return [(axis, step) for axis in range(3) for step in range(2) if sizes[axis] > 1 + step]


def is_even(axis):
    return lax.rem(lax.axis_index(AXES[axis]), 2) == 0


def pack_kernel(swaps, volume, *messages):
    depth, rows, cols = volume.shape
    lane = lax.broadcasted_iota(jnp.int32, (rows, cols), 1)
    for (axis, step), message in zip(swaps, messages):
        send_high = is_even(axis) if step == 0 else jnp.logical_not(is_even(axis))
        if axis == 0:
            message[...] = volume[jnp.where(send_high, depth - 1, 0)]
        elif axis == 1:
            message[...] = jnp.where(send_high, volume[:, rows - 1, :], volume[:, 0, :])
        else:
            packed = jnp.zeros((rows, cols), jnp.int32)
            for d in range(depth):
                shift = jnp.where(send_high, d + 1, d)
                packed = jnp.where(lane == d, pltpu.roll(volume[d], shift, 1), packed)
            message[...] = packed


def looked_up(table, channel, indices):
    rows = indices.shape[0]
    low = lax.rem(indices, LANES)
    result = None
    for start in range(0, table.shape[1], LANES):
        piece = jnp.broadcast_to(table[channel : channel + 1, start : start + LANES], (rows, LANES))
        found = jnp.take_along_axis(piece, low, axis=1, mode="promise_in_bounds")
        result = found if result is None else jnp.where(indices >= start, found, result)
    return result


def march_kernel(swaps, sizes, extent, volume, table, footprint, *refs):
    messages, partial = refs[:-1], refs[-1]
    depth, rows, cols = volume.shape
    lane = lax.broadcasted_iota(jnp.int32, (rows, cols), 1)
    row = lax.broadcasted_iota(jnp.int32, (rows, cols), 0)

    below = [jnp.zeros((rows, cols), jnp.float32), jnp.zeros((depth, cols), jnp.float32), jnp.zeros((rows, cols), jnp.float32)]
    above = list(below)
    for (axis, step), message in zip(swaps, messages):
        index = lax.axis_index(AXES[axis])
        neighbour_above = is_even(axis) if step == 0 else jnp.logical_not(is_even(axis))
        other = jnp.where(neighbour_above, index + 1, index - 1)
        present = (other >= 0) & (other < sizes[axis])
        found = looked_up(table, 3, message[...])
        above[axis] = jnp.where(neighbour_above & present, found, above[axis])
        below[axis] = jnp.where(jnp.logical_not(neighbour_above) & present, found, below[axis])

    density = [looked_up(table, 3, volume[d]) for d in range(depth)]
    colour = [jnp.zeros((rows, cols), jnp.float32) for _ in range(3)]
    transmit = jnp.ones((rows, cols), jnp.float32)
    for d in range(depth):
        centre = density[d]
        low = density[d - 1] if d > 0 else below[0]
        high = density[d + 1] if d < depth - 1 else above[0]
        grad_x = 0.5 * (high - low)
        low = jnp.where(row == 0, below[1][d : d + 1, :], pltpu.roll(centre, 1, 0))
        high = jnp.where(row == rows - 1, above[1][d : d + 1, :], pltpu.roll(centre, rows - 1, 0))
        grad_y = 0.5 * (high - low)
        low = jnp.where(lane == 0, pltpu.roll(below[2], (cols - d) % cols, 1), pltpu.roll(centre, 1, 1))
        high = jnp.where(lane == cols - 1, pltpu.roll(above[2], cols - 1 - d, 1), pltpu.roll(centre, cols - 1, 1))
        grad_z = 0.5 * (high - low)
        dot = grad_x * LIGHT[0] + grad_y * LIGHT[1] + grad_z * LIGHT[2]
        norm = 1.0 + (grad_x * grad_x + grad_y * grad_y + grad_z * grad_z)
        shading = 0.35 + 0.65 * (jnp.abs(dot) * lax.rsqrt(norm))
        sample_alpha = 1.0 - jnp.exp(-extent * centre)
        weight = transmit * sample_alpha * shading
        for c in range(3):
            colour[c] = colour[c] + weight * looked_up(table, c, volume[d])
        transmit = transmit * (1.0 - sample_alpha)

    inside = (row >= footprint[0]) & (row < footprint[1]) & (lane >= footprint[2]) & (lane < footprint[3])
    for c in range(3):
        partial[c] = jnp.where(inside, colour[c], 0.0)
    partial[3] = jnp.where(inside, transmit, 1.0)


def blend_kernel(count, ranks, *refs):
    layers, out = refs[:-1], refs[-1]
    me = lax.axis_index(AXES[0])
    rank = [ranks[lax.rem(me + k, count)] for k in range(count)]
    transmit = [layer[3] for layer in layers]
    colour = [jnp.zeros(transmit[0].shape, jnp.float32) for _ in range(3)]
    for i in range(count):
        cover = jnp.ones(transmit[0].shape, jnp.float32)
        for j in range(count):
            if j != i:
                cover = cover * jnp.where(rank[j] < rank[i], transmit[j], 1.0)
        for c in range(3):
            colour[c] = colour[c] + cover * layers[i][c]
    through = functools.reduce(lambda a, b: a * b, transmit)
    for c in range(3):
        out[c] = colour[c]
    out[3] = 1.0 - through


VMEM = pl.BlockSpec(memory_space=pltpu.VMEM)
SMEM = pl.BlockSpec(memory_space=pltpu.SMEM)
PARAMS = pltpu.CompilerParams(vmem_limit_bytes=SMALL_VMEM)


def cost(flops):
    return pl.CostEstimate(flops=flops, bytes_accessed=1 << 16, transcendentals=0)


def on_device(volume, transfer_table, depth_rank, footprint):
    depth, rows, cols = volume.shape
    sizes = tuple(lax.axis_size(name) for name in AXES)
    extent = 4.0 / (depth * sizes[0])
    swaps = swaps_of(sizes)

    shapes = [(depth, cols) if axis == 1 else (rows, cols) for axis, _ in swaps]
    messages = pl.pallas_call(
        functools.partial(pack_kernel, swaps),
        out_shape=[jax.ShapeDtypeStruct(shape, jnp.int32) for shape in shapes],
        in_specs=[VMEM],
        out_specs=[VMEM] * len(swaps),
        compiler_params=PARAMS,
        cost_estimate=cost(1 << 20),
        name="pack",
    )(volume)
    received = [
        lax.ppermute(message, AXES, swap_pairs(sizes, axis, step))
        for (axis, step), message in zip(swaps, messages)
    ]

    image = jax.ShapeDtypeStruct((4, rows, cols), jnp.float32)
    partial = pl.pallas_call(
        functools.partial(march_kernel, swaps, sizes, extent),
        out_shape=image,
        in_specs=[VMEM, VMEM, SMEM] + [VMEM] * len(swaps),
        out_specs=VMEM,
        compiler_params=PARAMS,
        cost_estimate=cost(1 << 22),
        name="march",
    )(volume, transfer_table, footprint.reshape(4), *received)

    count = sizes[0]
    layers = [partial] + [
        lax.ppermute(partial, AXES[0], [((i + k) % count, i) for i in range(count)]) for k in range(1, count)
    ]
    return pl.pallas_call(
        functools.partial(blend_kernel, count),
        out_shape=image,
        in_specs=[SMEM] + [VMEM] * count,
        out_specs=VMEM,
        compiler_params=PARAMS,
        cost_estimate=cost(1 << 20),
        name="blend",
    )(depth_rank, *layers)


def solution(mesh):
    placed = (P("gx", "gy", "gz"), P(), P(), P("gx", "gy", "gz", None))
    return jax.shard_map(
        on_device, mesh=mesh, in_specs=placed, out_specs=P(None, "gy", "gz"), check_vma=False
    )
```

time: 138 us -> 19.5 us (0.14)
  local copies, waits for them, and re-layouts: 67 us -> 0.85 us
  loops' own time: 25.6 us -> 0 us
  blocking collectives: 14.8 us -> 0 us
  other arithmetic: 7.12 us -> 0 us
  waiting for transfers between devices: 9.22 us -> 4.38 us
  Pallas kernels: 0 us -> 2.44 us
  starting transfers between devices: 13.6 us -> 11.7 us
    gather x3 -> x0, local copies, waits for them, and re-layouts: 60.3 us -> none  [the longest x2 59.7 us: on_device(): looked = jnp.take(transfer_table, volume, axis=1)]
    another operation x2 -> x0, loops' own time: 25.6 us -> none  [the longest x1 25.5 us: on_device(): lax.scan(advance, start_pair, jnp.arange(slab_depth, dtype=jnp.int32))]
    all_gather x1 -> x0, blocking collectives: 14.8 us -> none  [on_device(): layers = lax.all_gather(partial_value, 'gx', axis=0, tiled=True)]
    dynamic_slice x8 -> x0, local copies, waits for them, and re-layouts: 5.09 us -> none  [on_device(): lax.scan(advance, start_pair, jnp.arange(slab_depth, dtype=jnp.int32))]
    ppermute x6 -> x8, waiting for transfers between devices: 9.22 us -> 4.38 us  [the longest x3 2.72 us: on_device(): lax.ppermute(partial, AXES[0], [((i + k) % count, i) for i in range(count)])]
    pallas_call x0 -> x3, Pallas kernels: none -> 2.44 us  [the longest x1 1.19 us: on_device(): pl.pallas_call(functools.partial(blend_kernel, count), out_shape=image, i...]
    and x4 -> x0, other arithmetic: 2.22 us -> none  [the longest x2 1.35 us: on_device(): (rows_local >= rect[0]) & (rows_local < rect[1]) & (cols_local >= rect[2])]
    ppermute x6 -> x8, starting transfers between devices: 13.6 us -> 11.7 us  [the longest x5 6.25 us: on_device(): lax.ppermute(message, AXES, swap_pairs(sizes, axis, step))]
  transfers between devices with their start and end apart: 6 -> 8, of which waited for: 4 -> 3; matrix products, arithmetic and copies ran while one was open for 3% -> 0% of each run, Pallas kernels for 0% -> 0%
where the time goes in v1:
time: 19.5 us; the launch traced here: 19.4 us
  starting transfers between devices  11.7 us (60%)
  waiting for transfers between devices  4.38 us (22%)
  Pallas kernels  2.44 us (13%)
  local copies, waits for them, and re-layouts  0.85 us (4%)
    ppermute x5, starting transfers between devices, on_device(): lax.ppermute(message, AXES, swap_pairs(sizes, axis, step))  6.25 us
    ppermute x3, starting transfers between devices, on_device(): lax.ppermute(partial, AXES[0], [((i + k) % count, i) for i in range(count)])  5.42 us
    ppermute x3, waiting for transfers between devices, on_device(): lax.ppermute(partial, AXES[0], [((i + k) % count, i) for i in range(count)])  2.72 us
    ppermute x5, waiting for transfers between devices, on_device(): lax.ppermute(message, AXES, swap_pairs(sizes, axis, step))  1.66 us
    pallas_call x1, Pallas kernels, on_device(): pl.pallas_call(functools.partial(blend_kernel, count), out_shape=image, i...  1.19 us
    pallas_call x1, Pallas kernels, on_device(): pl.pallas_call(functools.partial(march_kernel, swaps, sizes, extent), out...  1.16 us
    unnamed x8, local copies, waits for them, and re-layouts  0.85 us
  transfers between devices with their start and end apart: 8, of which 3 were waited for; matrix products, arithmetic and copies ran while one was open for 0% of the time, Pallas kernels for 0%

profile of v1, /device:TPU:0, one launch (start us, length us, event | category | flops | bytes accessed | tf_op | source)
XLA Modules:
  0.0 19.4 jit_solution(9094783223767189706)
XLA Ops:
  0.0 0.0 copy-start
  0.0 0.8 %copy-done = s32[8,16,128]{2,1,0:T(8,128)S(1)} copy-done((s32[8,16,128]{2,1,0:T(8,128)S(1)}, s32[8,16,128]{2,1,0:T(8,128)}, u32[]{:S(2)}) %copy-start) | copy-done | bytes 65560
  0.8 0.1 pack.1
  0.9 3.1 %collective-permute-start = (s32[16,128]{1,0:T(8,128)S(1)}, s32[16,128]{1,0:T(8,128)S(1)}, u32[]{:S(2)}, u32[]{:S(2)}) collective-permute-start(s32[16,128]{1,0:T(8,128)S(1)} %get-tuple-element.10), channel_id=1, source_target_pairs={{0,8},{1,9},{2,10},{3,11},{4,12},{5,13},{6,14},{7,15},{8,0},{9,1},... | collective-permute-start | bytes 24584 | tf_op jit(solution)/shard_map/ppermute | solution.py:167
  4.1 0.0 copy-start.1
  4.1 0.0 collective-permute-start.1
  4.1 1.5 %collective-permute-start.4 = (s32[16,128]{1,0:T(8,128)S(1)}, s32[16,128]{1,0:T(8,128)S(1)}, u32[]{:S(2)}, u32[]{:S(2)}) collective-permute-start(s32[16,128]{1,0:T(8,128)S(1)} %get-tuple-element.14), channel_id=1, source_target_pairs={{0,1},{1,0},{2,3},{3,2},{4,5},{5,4},{6,7},{7,6},{8,9},{9,8},{10,11... | collective-permute-start | bytes 24584 | tf_op jit(solution)/shard_map/ppermute | solution.py:167
  5.6 0.2 %collective-permute-start.2 = (s32[8,128]{1,0:T(8,128)S(1)}, s32[8,128]{1,0:T(8,128)S(1)}, u32[]{:S(2)}, u32[]{:S(2)}) collective-permute-start(s32[8,128]{1,0:T(8,128)S(1)} %get-tuple-element.12), channel_id=1, source_target_pairs={{0,2},{1,3},{2,0},{3,1},{4,6},{5,7},{6,4},{7,5},{8,10},{9,11},{10,... | collective-permute-start | bytes 12296 | tf_op jit(solution)/shard_map/ppermute | solution.py:167
  5.8 0.0 copy-start.2
  5.8 1.4 %collective-permute-start.3 = (s32[8,128]{1,0:T(8,128)S(1)}, s32[8,128]{1,0:T(8,128)S(1)}, u32[]{:S(2)}, u32[]{:S(2)}) collective-permute-start(s32[8,128]{1,0:T(8,128)S(1)} %get-tuple-element.13), channel_id=1, source_target_pairs={{0,6},{1,7},{2,4},{3,5},{4,2},{5,3},{6,0},{7,1},{8,14},{9,15},{10,... | collective-permute-start | bytes 12296 | tf_op jit(solution)/shard_map/ppermute | solution.py:167
  7.2 0.0 collective-permute-done.2.refs_2_
  7.2 1.7 %collective-permute-done.3.refs_3_ = s32[8,128]{1,0:T(8,128)S(1)} collective-permute-done((s32[8,128]{1,0:T(8,128)S(1)}, s32[8,128]{1,0:T(8,128)S(1)}, u32[]{:S(2)}, u32[]{:S(2)}) %collective-permute-start.3) | collective-permute-done | bytes 4128 | tf_op jit(solution)/shard_map/ppermute | solution.py:167
  8.8 0.0 collective-permute-done.refs_0_
  8.8 0.0 collective-permute-done.1.refs_1_
  8.8 0.0 collective-permute-done.4.refs_4_
  8.9 0.0 copy-done.1
  8.9 0.0 copy-done.2
  8.9 0.0 copy-start.3
  8.9 1.2 %march.1.refs_0_ = f32[4,16,128]{2,1,0:T(8,128)S(1)} custom-call(s32[8,16,128]{2,1,0:T(8,128)S(1)} %copy-done, f32[4,256]{1,0:T(4,128)S(1)} %copy-done.1, s32[4]{0:T(128)S(1)} %bitcast.1, s32[16,128]{1,0:T(8,128)S(1)} %collective-permute-done.refs_0_, s32[16,128]{1,0:T(8,128)S(1)} %collective-permute-done.1.refs_1_, ...), custom_call_target="tpu_custom_call" | custom-call | flops 4194304 | bytes 65536 | tf_op jit(solution)/shard_map/march/pallas_call | solution.py:172
  10.1 3.0 %collective-permute-start.7 = (f32[4,16,128]{2,1,0:T(8,128)S(1)}, f32[4,16,128]{2,1,0:T(8,128)S(1)}, u32[]{:S(2)}, u32[]{:S(2)}) collective-permute-start(f32[4,16,128]{2,1,0:T(8,128)S(1)} %march.1.refs_0_), channel_id=1, source_target_pairs={{24,0},{0,8},{8,16},{16,24},{25,1},{1,9},{9,17},{17,25},{26,2},{2,... | collective-permute-start | bytes 98312 | tf_op jit(solution)/shard_map/ppermute | solution.py:184
  13.0 0.1 collective-permute-start.6
  13.1 2.3 %collective-permute-start.5 = (f32[4,16,128]{2,1,0:T(8,128)S(1)}, f32[4,16,128]{2,1,0:T(8,128)S(1)}, u32[]{:S(2)}, u32[]{:S(2)}) collective-permute-start(f32[4,16,128]{2,1,0:T(8,128)S(1)} %march.1.refs_0_), channel_id=1, source_target_pairs={{8,0},{16,8},{24,16},{0,24},{9,1},{17,9},{25,17},{1,25},{10,2},{18... | collective-permute-start | bytes 98312 | tf_op jit(solution)/shard_map/ppermute | solution.py:184
  15.5 0.3 %collective-permute-done.7.refs_3_ = f32[4,16,128]{2,1,0:T(8,128)S(1)} collective-permute-done((f32[4,16,128]{2,1,0:T(8,128)S(1)}, f32[4,16,128]{2,1,0:T(8,128)S(1)}, u32[]{:S(2)}, u32[]{:S(2)}) %collective-permute-start.7) | collective-permute-done | bytes 32800 | tf_op jit(solution)/shard_map/ppermute | solution.py:184
  15.8 2.4 %collective-permute-done.6.refs_2_ = f32[4,16,128]{2,1,0:T(8,128)S(1)} collective-permute-done((f32[4,16,128]{2,1,0:T(8,128)S(1)}, f32[4,16,128]{2,1,0:T(8,128)S(1)}, u32[]{:S(2)}, u32[]{:S(2)}) %collective-permute-start.6) | collective-permute-done | bytes 32800 | tf_op jit(solution)/shard_map/ppermute | solution.py:184
  18.2 0.0 collective-permute-done.5.refs_1_
  18.2 0.0 copy-done.3
  18.2 1.2 %blend.1 = f32[4,16,128]{2,1,0:T(8,128)} custom-call(s32[4]{0:T(128)S(1)} %copy-done.3, f32[4,16,128]{2,1,0:T(8,128)S(1)} %march.1.refs_0_, f32[4,16,128]{2,1,0:T(8,128)S(1)} %collective-permute-done.5.refs_1_, f32[4,16,128]{2,1,0:T(8,128)S(1)} %collective-permute-done.6.refs_2_, f32[4,16,128]{2,1,0:T(8,128)S(1)} %collective-permute-done.7.refs_3_), custom_call_target="tpu_custom_call" | custom-call | flops 1048576 | bytes 65536 | tf_op jit(solution)/shard_map/blend/pallas_call | solution.py:186
Async XLA Ops:
  0.0 0.8 %copy-start = (s32[8,16,128]{2,1,0:T(8,128)S(1)}, s32[8,16,128]{2,1,0:T(8,128)}, u32[]{:S(2)}) copy-start(s32[8,16,128]{2,1,0:T(8,128)} %volume.3) | copy-start | bytes 196612
  0.9 7.9 %collective-permute-start = (s32[16,128]{1,0:T(8,128)S(1)}, s32[16,128]{1,0:T(8,128)S(1)}, u32[]{:S(2)}, u32[]{:S(2)}) collective-permute-start(s32[16,128]{1,0:T(8,128)S(1)} %get-tuple-element.10), channel_id=1, source_target_pairs={{0,8},{1,9},{2,10},{3,11},{4,12},{5,13},{6,14},{7,15},{8,0},{9,1},... | collective-permute-start | bytes 24584 | tf_op jit(solution)/shard_map/ppermute | solution.py:167
  4.1 4.8 %copy-start.1 = (f32[4,256]{1,0:T(4,128)S(1)}, f32[4,256]{1,0:T(4,128)}, u32[]{:S(2)}) copy-start(f32[4,256]{1,0:T(4,128)} %table.1) | copy-start | bytes 12292
  4.1 4.8 %collective-permute-start.1 = (s32[16,128]{1,0:T(8,128)S(1)}, s32[16,128]{1,0:T(8,128)S(1)}, u32[]{:S(2)}, u32[]{:S(2)}) collective-permute-start(s32[16,128]{1,0:T(8,128)S(1)} %get-tuple-element.11), channel_id=1, source_target_pairs={{0,2},{1,3},{2,0},{3,1},{4,6},{5,7},{6,4},{7,5},{8,16},{9,17},{10,... | collective-permute-start | bytes 24584 | tf_op jit(solution)/shard_map/ppermute | solution.py:167
  4.1 4.8 %collective-permute-start.4 = (s32[16,128]{1,0:T(8,128)S(1)}, s32[16,128]{1,0:T(8,128)S(1)}, u32[]{:S(2)}, u32[]{:S(2)}) collective-permute-start(s32[16,128]{1,0:T(8,128)S(1)} %get-tuple-element.14), channel_id=1, source_target_pairs={{0,1},{1,0},{2,3},{3,2},{4,5},{5,4},{6,7},{7,6},{8,9},{9,8},{10,11... | collective-permute-start | bytes 24584 | tf_op jit(solution)/shard_map/ppermute | solution.py:167
  5.6 1.6 %collective-permute-start.2 = (s32[8,128]{1,0:T(8,128)S(1)}, s32[8,128]{1,0:T(8,128)S(1)}, u32[]{:S(2)}, u32[]{:S(2)}) collective-permute-start(s32[8,128]{1,0:T(8,128)S(1)} %get-tuple-element.12), channel_id=1, source_target_pairs={{0,2},{1,3},{2,0},{3,1},{4,6},{5,7},{6,4},{7,5},{8,10},{9,11},{10,... | collective-permute-start | bytes 12296 | tf_op jit(solution)/shard_map/ppermute | solution.py:167
  5.8 3.1 %copy-start.2 = (s32[1,1,1,4]{3,2,1,0:T(1,128)S(1)}, s32[1,1,1,4]{3,2,1,0:T(1,128)}, u32[]{:S(2)}) copy-start(s32[1,1,1,4]{3,2,1,0:T(1,128)} %param.7) | copy-start | bytes 52
  5.8 3.0 %collective-permute-start.3 = (s32[8,128]{1,0:T(8,128)S(1)}, s32[8,128]{1,0:T(8,128)S(1)}, u32[]{:S(2)}, u32[]{:S(2)}) collective-permute-start(s32[8,128]{1,0:T(8,128)S(1)} %get-tuple-element.13), channel_id=1, source_target_pairs={{0,6},{1,7},{2,4},{3,5},{4,2},{5,3},{6,0},{7,1},{8,14},{9,15},{10,... | collective-permute-start | bytes 12296 | tf_op jit(solution)/shard_map/ppermute | solution.py:167
  8.9 9.3 %copy-start.3 = (s32[4]{0:T(128)S(1)}, s32[4]{0:T(128)}, u32[]{:S(2)}) copy-start(s32[4]{0:T(128)} %ranks.1) | copy-start | bytes 52
  10.1 5.8 %collective-permute-start.7 = (f32[4,16,128]{2,1,0:T(8,128)S(1)}, f32[4,16,128]{2,1,0:T(8,128)S(1)}, u32[]{:S(2)}, u32[]{:S(2)}) collective-permute-start(f32[4,16,128]{2,1,0:T(8,128)S(1)} %march.1.refs_0_), channel_id=1, source_target_pairs={{24,0},{0,8},{8,16},{16,24},{25,1},{1,9},{9,17},{17,25},{26,2},{2,... | collective-permute-start | bytes 98312 | tf_op jit(solution)/shard_map/ppermute | solution.py:184
  13.0 5.2 %collective-permute-start.6 = (f32[4,16,128]{2,1,0:T(8,128)S(1)}, f32[4,16,128]{2,1,0:T(8,128)S(1)}, u32[]{:S(2)}, u32[]{:S(2)}) collective-permute-start(f32[4,16,128]{2,1,0:T(8,128)S(1)} %march.1.refs_0_), channel_id=1, source_target_pairs={{16,0},{24,8},{0,16},{8,24},{17,1},{25,9},{1,17},{9,25},{18,2},{26... | collective-permute-start | bytes 98312 | tf_op jit(solution)/shard_map/ppermute | solution.py:184
  13.1 5.0 %collective-permute-start.5 = (f32[4,16,128]{2,1,0:T(8,128)S(1)}, f32[4,16,128]{2,1,0:T(8,128)S(1)}, u32[]{:S(2)}, u32[]{:S(2)}) collective-permute-start(f32[4,16,128]{2,1,0:T(8,128)S(1)} %march.1.refs_0_), channel_id=1, source_target_pairs={{8,0},{16,8},{24,16},{0,24},{9,1},{17,9},{25,17},{1,25},{10,2},{18... | collective-permute-start | bytes 98312 | tf_op jit(solution)/shard_map/ppermute | solution.py:184
